TPU v7x, 32 devices: a whole 2x2x4 slice. The times are simulated.
32 devices in a mesh: tm: 16 (over z, y, x), rows: 2 (over core).
Axes of the slice: x: 2, y: 2, z: 4, core: 2. Of those that a mesh axis runs over, the one named last changes fastest.
Arguments:
- resid: float32 [2, 16, 16, 512], P(None, 'tm', 'rows'), may hold values from -3 to 3
- basis: float32 [4, 2, 16, 16, 512], P(None, None, 'tm', 'rows'), may hold values from -0.01171875 to 0.01171875
Outputs:
- precond: float32 [2, 16, 16, 512], P(None, 'tm', 'rows')
- image: float32 [2, 16, 16, 512], P(None, 'tm', 'rows')
- gram: float32 [5], replicated
All inputs are finite; a program needn't handle non-finite values.
Results may differ from a plain program's by a relative error of at most 0.0005.
Values sent between devices are 32-bit elements; how exact they have to be, the bound alone decides.
A program may use at most 64 MiB of HBM per device.

v0:
```python
import math
import jax
import jax.numpy as jnp
from jax import lax
from jax.sharding import PartitionSpec as P

SWEEPS = 4
ALPHA = 0.01


def padded_2(shard, sides, width):
    for axis, dim in sides:
        count, length = (lax.axis_size(axis), shard.shape[dim])
        up = [(i, (i + 1) % count) for i in range(count - 1)]
        down = [(j, i) for i, j in up]
        last = lax.slice_in_dim(shard, length - width, length, axis=dim)
        first = lax.slice_in_dim(shard, 0, width, axis=dim)
        before = lax.ppermute(last, axis, up)
        after = lax.ppermute(first, axis, down)
        shard = jnp.concatenate([before, shard, after], axis=dim)
    return shard


def shifted(value, axis, steps):
    count = lax.axis_size(axis)
    first, last = (max(0, -steps), min(count, count - steps))
    return lax.ppermute(value, axis, [(source, source + steps) for source in range(first, last)])


def neighbours(padded):
    middle = padded[:, 1:-1]
    sides = jnp.pad(middle, ((0, 0), (0, 0), (1, 1)))
    return padded[:, 2:] + padded[:, :-2] + sides[:, :, 2:] + sides[:, :, :-2]


def cmul(left, right_re, right_im):
    return jnp.stack(
        [left[0] * right_re - left[1] * right_im, left[0] * right_im + left[1] * right_re]
    )


def phases(first, second, steps):
    turns = first * second % steps
    angle = turns.astype(jnp.float32) * (2.0 * math.pi / steps)
    return (jnp.cos(angle), jnp.sin(angle))


def on_device(resid, basis):
    steps = lax.axis_size("tm")
    coupling = 16.0 / (steps * steps)
    me = lax.axis_index("tm")
    rows_dev = resid.shape[2]
    cols = resid.shape[3]
    cells = rows_dev * cols
    piece = cells // steps
    mine = me.astype(jnp.float32)
    gamma = jnp.power(jnp.float32(ALPHA), mine / steps)
    scaled = resid[:, 0] * gamma
    ordinal = jnp.arange(steps, dtype=jnp.int32)
    cos_table, sin_table = phases(ordinal[:, None], ordinal[None, :], steps)
    blocks = lax.all_to_all(
        scaled.reshape(1, 2, cells), "tm", split_axis=2, concat_axis=0, tiled=True
    )
    flat = blocks.reshape(steps, 2 * piece)
    real_part = jnp.dot(cos_table, flat, precision=lax.Precision.HIGHEST)
    imag_part = -jnp.dot(sin_table, flat, precision=lax.Precision.HIGHEST)
    stacked = jnp.stack([real_part, imag_part], 1).reshape(steps, 2, 2, piece)
    spectrum = lax.all_to_all(stacked, "tm", split_axis=0, concat_axis=3, tiled=True)
    rhat = spectrum[0].reshape(2, 2, rows_dev, cols)
    base = jnp.power(jnp.float32(ALPHA), jnp.float32(1.0) / steps)
    angle = mine * (2.0 * math.pi / steps)
    lam_re = 1.0 - base * jnp.cos(angle)
    lam_im = base * jnp.sin(angle)
    disp_spec = rhat[:, 0]
    right = cmul(disp_spec, lam_re, lam_im) + rhat[:, 1]
    den_re = lam_re * lam_re - lam_im * lam_im + 4.0 * coupling
    den_im = 2.0 * lam_re * lam_im
    magnitude = den_re * den_re + den_im * den_im
    inv_re = den_re / magnitude
    inv_im = -den_im / magnitude
    uhat = cmul(right, inv_re, inv_im)
    for sweep in range(SWEEPS - 1):
        padded = padded_2(uhat, (("rows", 1),), 1)
        uhat = cmul(right + coupling * neighbours(padded), inv_re, inv_im)
    vhat = cmul(uhat, lam_re, lam_im) - disp_spec
    yhat = jnp.stack([uhat, vhat], 1)
    spread = lax.all_to_all(
        yhat.reshape(1, 2, 2, cells), "tm", split_axis=3, concat_axis=0, tiled=True
    )
    real_rows = spread[:, 0].reshape(steps, 2 * piece)
    imag_rows = spread[:, 1].reshape(steps, 2 * piece)
    undo = jnp.power(jnp.float32(ALPHA), -ordinal.astype(jnp.float32) / steps) / steps
    history = jnp.dot(cos_table, real_rows, precision=lax.Precision.HIGHEST) - jnp.dot(
        sin_table, imag_rows, precision=lax.Precision.HIGHEST
    )
    history = (history * undo[:, None]).reshape(steps, 2, piece)
    returned = lax.all_to_all(history, "tm", split_axis=0, concat_axis=2, tiled=True)
    precond = returned[0].reshape(2, rows_dev, cols)
    earlier = shifted(precond, "tm", 1)
    disp_rim = padded_2(precond[0:1], (("rows", 1),), 1)
    laplace = neighbours(disp_rim)[0] - 4.0 * precond[0]
    first = precond[0] - earlier[0] - precond[1]
    second = precond[1] - earlier[1] - coupling * laplace
    image = jnp.stack([first, second])
    inner = jnp.sum(basis[:, :, 0] * image[None], axis=(1, 2, 3))
    count = 2.0 * steps * rows_dev * lax.axis_size("rows") * cols
    squares = jnp.sum(image * image) / count
    local_terms = jnp.concatenate([inner, squares[None]])
    gram = lax.psum(local_terms, ("tm", "rows"))
    return (precond[:, None], image[:, None], gram)


def solution(mesh):
    in_specs = (P(None, "tm", "rows", None), P(None, None, "tm", "rows", None))
    out_specs = (P(None, "tm", "rows", None), P(None, "tm", "rows", None), P())
    return jax.shard_map(
        on_device, mesh=mesh, in_specs=in_specs, out_specs=out_specs, check_vma=False
    )
```

profile of v0, /device:TPU:0, one launch (start us, length us, event | category | flops | bytes accessed | tf_op | source)
XLA Modules:
  0.0 169.4 jit_solution(10434036143663607024)
XLA Ops:
  0.7 0.8 broadcast_multiply_fusion
  1.4 0.6 copy.44
  2.1 0.5 broadcast.139
  2.6 19.4 %reduce.4 = f32[4096,2]{1,0:T(8,128)} reduce(f32[4096,1,2]{2,1,0:T(1,128)S(1)} %bitcast.83, f32[]{:T(128)} %broadcast.139), dimensions={1}, to_apply=%bitcast.65.reduce_sub_computation | reduce | bytes 65540
  22.0 3.0 %reshape.138 = f32[16,1,512]{2,1,0:T(1,128)S(1)} reshape(f32[4096,2]{1,0:T(8,128)} %reduce.4) | data formatting | bytes 65536
  25.0 15.5 %all_to_all.63 = f32[16,1,512]{2,1,0:T(1,128)S(1)} all-to-all(f32[16,1,512]{2,1,0:T(1,128)S(1)} %reshape.138), channel_id=1, replica_groups=mesh['tm'=16,'rows'=2] {'tm'}, dimensions={0} | all-to-all | bytes 65536 | tf_op jit(solution)/shard_map/all_to_all | solution.py:61
  40.5 0.7 reduce.5
  41.3 3.4 %reshape.139 = f32[4096,1,2]{2,1,0:T(1,128)S(1)} reshape(f32[16,512]{1,0:T(8,128)S(1)} %reduce.5) | data formatting | bytes 65536
  44.7 0.6 copy.45
  45.3 0.2 convolution_bitcast_fusion
  45.5 0.2 convolution_negate_fusion
  45.8 0.7 copy.48
  46.5 3.5 %all-to-all-start.1 = ((f32[16,2,2,256]{3,2,1,0:T(2,128)}), f32[16,2,2,256]{3,2,1,0:T(2,128)S(1)}, u32[]{:S(2)}, u32[]{:S(2)}) async-start(f32[16,2,2,256]{3,2,1,0:T(2,128)} %copy.48), calls=%async_computation.1 | async-start | bytes 131072 | tf_op jit(solution)/shard_map/all_to_all | solution.py:68
  50.2 7.2 %all-to-all-done.1 = f32[16,2,2,256]{3,2,1,0:T(2,128)S(1)} async-done(((f32[16,2,2,256]{3,2,1,0:T(2,128)}), f32[16,2,2,256]{3,2,1,0:T(2,128)S(1)}, u32[]{:S(2)}, u32[]{:S(2)}) %all-to-all-start.1) | async-done | bytes 65568 | tf_op jit(solution)/shard_map/all_to_all | solution.py:68
  57.6 1.3 collective-permute-start
  58.9 3.0 %collective-permute-start.1 = (f32[2,1,512]{2,1,0:T(1,128)S(1)}, f32[2,1,512]{2,1,0:T(1,128)S(1)}, u32[]{:S(2)}, u32[]{:S(2)}) collective-permute-start(f32[2,1,512]{2,1,0:T(1,128)S(1)} %get-tuple-element.26), channel_id=1, source_target_pairs={{0,1},{2,3},{4,5},{6,7},{8,9},{10,11},{12,13},{14,15},{16,17},{18,... | collective-permute-start | bytes 12296 | tf_op jit(solution)/shard_map/ppermute | solution.py:18
  61.9 0.0 collective-permute-done
  62.0 0.8 collective-permute-done.1
  62.7 0.1 fusion.5
  62.9 1.3 collective-permute-start.2
  64.2 3.0 %collective-permute-start.3 = (f32[2,1,512]{2,1,0:T(1,128)S(1)}, f32[2,1,512]{2,1,0:T(1,128)S(1)}, u32[]{:S(2)}, u32[]{:S(2)}) collective-permute-start(f32[2,1,512]{2,1,0:T(1,128)S(1)} %get-tuple-element.22), channel_id=1, source_target_pairs={{0,1},{2,3},{4,5},{6,7},{8,9},{10,11},{12,13},{14,15},{16,17},{18,... | collective-permute-start | bytes 12296 | tf_op jit(solution)/shard_map/ppermute | solution.py:18
  67.2 0.0 collective-permute-done.2
  67.2 0.8 collective-permute-done.3
  68.0 0.1 fusion.9
  68.1 1.3 collective-permute-start.4
  69.4 3.2 %collective-permute-start.5 = (f32[2,1,512]{2,1,0:T(1,128)S(1)}, f32[2,1,512]{2,1,0:T(1,128)S(1)}, u32[]{:S(2)}, u32[]{:S(2)}) collective-permute-start(f32[2,1,512]{2,1,0:T(1,128)S(1)} %get-tuple-element.18), channel_id=1, source_target_pairs={{0,1},{2,3},{4,5},{6,7},{8,9},{10,11},{12,13},{14,15},{16,17},{18,... | collective-permute-start | bytes 12296 | tf_op jit(solution)/shard_map/ppermute | solution.py:18
  72.6 0.0 collective-permute-done.4
  72.7 0.6 collective-permute-done.5
  73.3 0.1 fusion.13
  73.5 4.4 %copy.51 = f32[1,2,2,4096]{2,1,0,3:T(2,128)} copy(f32[1,2,2,4096]{3,1,2,0:T(2,128)S(1)} %pad_maximum_fusion.1) | data formatting | bytes 131072 | tf_op jit(solution)/shard_map/stack | solution.py:86
  77.9 8.1 %reshape.140 = f32[16,1,1024]{2,1,0:T(1,128)} reshape(f32[4096,1,2,2]{3,2,1,0:T(2,128)} %bitcast.81) | data formatting | bytes 131072
  86.0 3.5 %all-to-all-start.2 = ((f32[16,1,1024]{2,1,0:T(1,128)}), f32[16,1,1024]{2,1,0:T(1,128)S(1)}, u32[]{:S(2)}, u32[]{:S(2)}) async-start(f32[16,1,1024]{2,1,0:T(1,128)} %reshape.140), calls=%async_computation.2 | async-start | bytes 131072 | tf_op jit(solution)/shard_map/all_to_all | solution.py:87
  89.5 7.5 %all-to-all-done.2 = f32[16,1,1024]{2,1,0:T(1,128)S(1)} async-done(((f32[16,1,1024]{2,1,0:T(1,128)}), f32[16,1,1024]{2,1,0:T(1,128)S(1)}, u32[]{:S(2)}, u32[]{:S(2)}) %all-to-all-start.2) | async-done | bytes 65568 | tf_op jit(solution)/shard_map/all_to_all | solution.py:87
  97.0 0.8 reduce.6
  97.8 7.7 %reshape.141 = f32[4096,1,2,2]{3,2,1,0:T(2,128)} reshape(f32[16,1024]{1,0:T(8,128)S(1)} %reduce.6) | data formatting | bytes 131072
  105.6 0.0 copy-start
  105.6 3.6 %copy.57 = f32[1,2,2,16,256]{4,3,2,1,0:T(8,128)S(1)} copy(f32[1,2,2,16,256]{2,1,4,3,0:T(2,128)} %bitcast.82) | data formatting | bytes 131072 | tf_op jit(solution)/shard_map/all_to_all | solution.py:87
  109.2 0.2 fusion.42
  109.5 0.2 fusion
  109.7 10.0 %all_to_all.64 = f32[16,2,256]{2,1,0:T(2,128)S(1)} all-to-all(f32[16,2,256]{2,1,0:T(2,128)S(1)} %reshape.134), channel_id=1, replica_groups=mesh['tm'=16,'rows'=2] {'tm'}, dimensions={0} | all-to-all | bytes 65536 | tf_op jit(solution)/shard_map/all_to_all | solution.py:97
  119.7 0.1 slice_reduce_fusion
  119.8 2.6 %collective-permute-start.6 = (f32[2,8,512]{2,1,0:T(8,128)S(1)}, f32[2,8,512]{2,1,0:T(8,128)S(1)}, u32[]{:S(2)}, u32[]{:S(2)}) collective-permute-start(f32[2,8,512]{2,1,0:T(8,128)S(1)} %reshape_squeeze.15), channel_id=1, source_target_pairs={{0,2},{2,4},{4,6},{6,8},{8,10},{10,12},{12,14},{14,16},{16,18},{18... | collective-permute-start | bytes 98312 | tf_op jit(solution)/shard_map/ppermute | solution.py:27
  122.4 1.3 collective-permute-start.7
  123.7 3.0 %collective-permute-start.8 = (f32[1,1,512]{2,1,0:T(1,128)S(1)}, f32[1,1,512]{2,1,0:T(1,128)S(1)}, u32[]{:S(2)}, u32[]{:S(2)}) collective-permute-start(f32[1,1,512]{2,1,0:T(1,128)S(1)} %get-tuple-element.30), channel_id=1, source_target_pairs={{0,1},{2,3},{4,5},{6,7},{8,9},{10,11},{12,13},{14,15},{16,17},{18,... | collective-permute-start | bytes 6152 | tf_op jit(solution)/shard_map/ppermute | solution.py:18
  126.8 0.0 collective-permute-done.7
  126.8 0.8 collective-permute-done.8
  127.6 0.0 collective-permute-done.6
  127.6 0.1 fusion.26
  127.7 1.2 pad_maximum_fusion.18
  129.5 0.0 copy-done
  129.6 0.1 fusion.1
  129.7 0.1 pad_maximum_fusion.21
  129.8 0.6 broadcast_in_dim_reshape_squeeze.3
  130.4 39.0 %psum.7 = f32[5]{0:T(128)} all-reduce(f32[5]{0:T(128)S(1)} %pad_maximum_fusion.21), channel_id=1, replica_groups=mesh['tm'=16,'rows'=2] {'tm','rows'}, use_global_device_ids=true, to_apply=%region_2.3 | all-reduce | flops 5 | bytes 40 | tf_op jit(solution)/shard_map/psum | solution.py:109
  (36 shorter events, 0.4 us)
Async XLA Ops:
  46.5 11.0 %all-to-all-start.1 = ((f32[16,2,2,256]{3,2,1,0:T(2,128)}), f32[16,2,2,256]{3,2,1,0:T(2,128)S(1)}, u32[]{:S(2)}, u32[]{:S(2)}) async-start(f32[16,2,2,256]{3,2,1,0:T(2,128)} %copy.48), calls=%async_computation.1 | async-start | bytes 131072 | tf_op jit(solution)/shard_map/all_to_all | solution.py:68
  57.6 4.3 %collective-permute-start = (f32[2,1,512]{2,1,0:T(1,128)S(1)}, f32[2,1,512]{2,1,0:T(1,128)S(1)}, u32[]{:S(2)}, u32[]{:S(2)}) collective-permute-start(f32[2,1,512]{2,1,0:T(1,128)S(1)} %get-tuple-element.25), channel_id=1, source_target_pairs={{1,0},{3,2},{5,4},{7,6},{9,8},{11,10},{13,12},{15,14},{17,16},{19,... | collective-permute-start | bytes 12296 | tf_op jit(solution)/shard_map/ppermute | solution.py:19
  58.9 3.8 %collective-permute-start.1 = (f32[2,1,512]{2,1,0:T(1,128)S(1)}, f32[2,1,512]{2,1,0:T(1,128)S(1)}, u32[]{:S(2)}, u32[]{:S(2)}) collective-permute-start(f32[2,1,512]{2,1,0:T(1,128)S(1)} %get-tuple-element.26), channel_id=1, source_target_pairs={{0,1},{2,3},{4,5},{6,7},{8,9},{10,11},{12,13},{14,15},{16,17},{18,... | collective-permute-start | bytes 12296 | tf_op jit(solution)/shard_map/ppermute | solution.py:18
  62.9 4.3 %collective-permute-start.2 = (f32[2,1,512]{2,1,0:T(1,128)S(1)}, f32[2,1,512]{2,1,0:T(1,128)S(1)}, u32[]{:S(2)}, u32[]{:S(2)}) collective-permute-start(f32[2,1,512]{2,1,0:T(1,128)S(1)} %get-tuple-element.21), channel_id=1, source_target_pairs={{1,0},{3,2},{5,4},{7,6},{9,8},{11,10},{13,12},{15,14},{17,16},{19,... | collective-permute-start | bytes 12296 | tf_op jit(solution)/shard_map/ppermute | solution.py:19
  64.2 3.8 %collective-permute-start.3 = (f32[2,1,512]{2,1,0:T(1,128)S(1)}, f32[2,1,512]{2,1,0:T(1,128)S(1)}, u32[]{:S(2)}, u32[]{:S(2)}) collective-permute-start(f32[2,1,512]{2,1,0:T(1,128)S(1)} %get-tuple-element.22), channel_id=1, source_target_pairs={{0,1},{2,3},{4,5},{6,7},{8,9},{10,11},{12,13},{14,15},{16,17},{18,... | collective-permute-start | bytes 12296 | tf_op jit(solution)/shard_map/ppermute | solution.py:18
  68.1 4.5 %collective-permute-start.4 = (f32[2,1,512]{2,1,0:T(1,128)S(1)}, f32[2,1,512]{2,1,0:T(1,128)S(1)}, u32[]{:S(2)}, u32[]{:S(2)}) collective-permute-start(f32[2,1,512]{2,1,0:T(1,128)S(1)} %get-tuple-element.17), channel_id=1, source_target_pairs={{1,0},{3,2},{5,4},{7,6},{9,8},{11,10},{13,12},{15,14},{17,16},{19,... | collective-permute-start | bytes 12296 | tf_op jit(solution)/shard_map/ppermute | solution.py:19
  69.4 3.8 %collective-permute-start.5 = (f32[2,1,512]{2,1,0:T(1,128)S(1)}, f32[2,1,512]{2,1,0:T(1,128)S(1)}, u32[]{:S(2)}, u32[]{:S(2)}) collective-permute-start(f32[2,1,512]{2,1,0:T(1,128)S(1)} %get-tuple-element.18), channel_id=1, source_target_pairs={{0,1},{2,3},{4,5},{6,7},{8,9},{10,11},{12,13},{14,15},{16,17},{18,... | collective-permute-start | bytes 12296 | tf_op jit(solution)/shard_map/ppermute | solution.py:18
  86.0 11.0 %all-to-all-start.2 = ((f32[16,1,1024]{2,1,0:T(1,128)}), f32[16,1,1024]{2,1,0:T(1,128)S(1)}, u32[]{:S(2)}, u32[]{:S(2)}) async-start(f32[16,1,1024]{2,1,0:T(1,128)} %reshape.140), calls=%async_computation.2 | async-start | bytes 131072 | tf_op jit(solution)/shard_map/all_to_all | solution.py:87
  105.6 24.0 %copy-start = (f32[4,2,1,8,512]{4,3,2,1,0:T(8,128)S(1)}, f32[4,2,1,8,512]{4,3,2,1,0:T(8,128)}, u32[]{:S(2)}) copy-start(f32[4,2,1,8,512]{4,3,2,1,0:T(8,128)} %param.3) | copy-start | bytes 393220
  119.8 7.8 %collective-permute-start.6 = (f32[2,8,512]{2,1,0:T(8,128)S(1)}, f32[2,8,512]{2,1,0:T(8,128)S(1)}, u32[]{:S(2)}, u32[]{:S(2)}) collective-permute-start(f32[2,8,512]{2,1,0:T(8,128)S(1)} %reshape_squeeze.15), channel_id=1, source_target_pairs={{0,2},{2,4},{4,6},{6,8},{8,10},{10,12},{12,14},{14,16},{16,18},{18... | collective-permute-start | bytes 98312 | tf_op jit(solution)/shard_map/ppermute | solution.py:27
  122.4 4.4 %collective-permute-start.7 = (f32[1,1,512]{2,1,0:T(1,128)S(1)}, f32[1,1,512]{2,1,0:T(1,128)S(1)}, u32[]{:S(2)}, u32[]{:S(2)}) collective-permute-start(f32[1,1,512]{2,1,0:T(1,128)S(1)} %get-tuple-element.29), channel_id=1, source_target_pairs={{1,0},{3,2},{5,4},{7,6},{9,8},{11,10},{13,12},{15,14},{17,16},{19,... | collective-permute-start | bytes 6152 | tf_op jit(solution)/shard_map/ppermute | solution.py:19
  123.7 3.8 %collective-permute-start.8 = (f32[1,1,512]{2,1,0:T(1,128)S(1)}, f32[1,1,512]{2,1,0:T(1,128)S(1)}, u32[]{:S(2)}, u32[]{:S(2)}) collective-permute-start(f32[1,1,512]{2,1,0:T(1,128)S(1)} %get-tuple-element.30), channel_id=1, source_target_pairs={{0,1},{2,3},{4,5},{6,7},{8,9},{10,11},{12,13},{14,15},{16,17},{18,... | collective-permute-start | bytes 6152 | tf_op jit(solution)/shard_map/ppermute | solution.py:18
where the time goes:
time: 170 us; the launch traced here: 169 us
  blocking collectives  64.5 us (38%)
  local copies, waits for them, and re-layouts  33.7 us (20%)
  starting transfers between devices  27 us (16%)
  other arithmetic  23.6 us (14%)
  waiting for transfers between devices  17.7 us (10%)
  between operations  2.06 us (1%)
    psum x1, blocking collectives, on_device(): gram = lax.psum(local_terms, ('tm', 'rows'))  39 us
    unnamed x10, local copies, waits for them, and re-layouts  22.8 us
    unnamed x1, other arithmetic  19.4 us
    all_to_all x1, blocking collectives, on_device(): lax.all_to_all(scaled.reshape(1, 2, cells), 'tm', split_axis=2, concat_ax...  15.5 us
    ppermute x4, starting transfers between devices, padded_2(): before = lax.ppermute(last, axis, up)  12.3 us
    all_to_all x1, blocking collectives, on_device(): lax.all_to_all(history, 'tm', split_axis=0, concat_axis=2, tiled=True)  9.98 us
    all_to_all x1, waiting for transfers between devices, on_device(): lax.all_to_all(yhat.reshape(1, 2, 2, cells), 'tm', split_axis=3, concat_a...  7.49 us
    all_to_all x1, waiting for transfers between devices, on_device(): lax.all_to_all(stacked, 'tm', split_axis=0, concat_axis=3, tiled=True)  7.25 us
  transfers between devices with their start and end apart: 11, of which 6 were waited for; matrix products, arithmetic and copies ran while one was open for 0% of the time, Pallas kernels for 0%

commit v1 on v0

--- a/solution.py
+++ b/solution.py
@@ -6,6 +6,13 @@
 
 SWEEPS = 4
 ALPHA = 0.01
+
+
+def exchange_blocks(block, mesh_axis, split, join):
+    devices = lax.axis_size(mesh_axis)
+    pieces = jnp.stack(jnp.split(block, devices, axis=split), axis=0)
+    pieces = lax.all_to_all(pieces, mesh_axis, split_axis=0, concat_axis=0)
+    return jnp.concatenate(pieces, axis=join)
 
 
 def padded_2(shard, sides, width):
@@ -94,7 +101,7 @@
         sin_table, imag_rows, precision=lax.Precision.HIGHEST
     )
     history = (history * undo[:, None]).reshape(steps, 2, piece)
-    returned = lax.all_to_all(history, "tm", split_axis=0, concat_axis=2, tiled=True)
+    returned = exchange_blocks(history, "tm", 0, 2)
     precond = returned[0].reshape(2, rows_dev, cols)
     earlier = shifted(precond, "tm", 1)
     disp_rim = padded_2(precond[0:1], (("rows", 1),), 1)

time: 170 us -> 171 us (level)
    unnamed x10 -> x25, local copies, waits for them, and re-layouts: 22.8 us -> 22.9 us
where the time goes in v1:
time: 171 us; the launch traced here: 170 us
  blocking collectives  64.5 us (38%)
  local copies, waits for them, and re-layouts  34.1 us (20%)
  starting transfers between devices  27 us (16%)
  other arithmetic  23.6 us (14%)
  waiting for transfers between devices  17.7 us (10%)
  between operations  2.1 us (1%)
    psum x1, blocking collectives, on_device(): gram = lax.psum(local_terms, ('tm', 'rows'))  39 us
    unnamed x25, local copies, waits for them, and re-layouts  22.9 us
    unnamed x1, other arithmetic  19.4 us
    all_to_all x1, blocking collectives, on_device(): lax.all_to_all(scaled.reshape(1, 2, cells), 'tm', split_axis=2, concat_ax...  15.5 us
    ppermute x4, starting transfers between devices, padded_2(): before = lax.ppermute(last, axis, up)  12.3 us
    all_to_all x1, blocking collectives, exchange_blocks(): pieces = lax.all_to_all(pieces, mesh_axis, split_axis=0, concat_axis=0)  9.98 us
    all_to_all x1, waiting for transfers between devices, on_device(): lax.all_to_all(yhat.reshape(1, 2, 2, cells), 'tm', split_axis=3, concat_a...  7.49 us
    all_to_all x1, waiting for transfers between devices, on_device(): lax.all_to_all(stacked, 'tm', split_axis=0, concat_axis=3, tiled=True)  7.25 us
  transfers between devices with their start and end apart: 11, of which 6 were waited for; matrix products, arithmetic and copies ran while one was open for 0% of the time, Pallas kernels for 0%

profile of v1, /device:TPU:0, one launch (start us, length us, event | category | flops | bytes accessed | tf_op | source)
XLA Modules:
  0.0 169.9 jit_solution(18304846746218273440)
XLA Ops:
  0.7 0.8 broadcast_multiply_fusion
  1.4 0.6 copy.44
  2.1 0.5 broadcast.187
  2.6 19.4 %reduce.68 = f32[4096,2]{1,0:T(8,128)} reduce(f32[4096,1,2]{2,1,0:T(1,128)S(1)} %bitcast.81, f32[]{:T(128)} %broadcast.187), dimensions={1}, to_apply=%bitcast.63.reduce_sub_computation | reduce | bytes 65540
  22.0 3.0 %reshape.251 = f32[16,1,512]{2,1,0:T(1,128)S(1)} reshape(f32[4096,2]{1,0:T(8,128)} %reduce.68) | data formatting | bytes 65536
  25.0 15.5 %all_to_all.53 = f32[16,1,512]{2,1,0:T(1,128)S(1)} all-to-all(f32[16,1,512]{2,1,0:T(1,128)S(1)} %reshape.251), channel_id=1, replica_groups=mesh['tm'=16,'rows'=2] {'tm'}, dimensions={0} | all-to-all | bytes 65536 | tf_op jit(solution)/shard_map/all_to_all | solution.py:68
  40.6 0.7 reduce.69
  41.3 3.4 %reshape.252 = f32[4096,1,2]{2,1,0:T(1,128)S(1)} reshape(f32[16,512]{1,0:T(8,128)S(1)} %reduce.69) | data formatting | bytes 65536
  44.7 0.6 copy.45
  45.3 0.2 convolution_bitcast_fusion
  45.5 0.2 convolution_negate_fusion
  45.8 0.7 copy.48
  46.5 3.5 %all-to-all-start.1 = ((f32[16,2,2,256]{3,2,1,0:T(2,128)}), f32[16,2,2,256]{3,2,1,0:T(2,128)S(1)}, u32[]{:S(2)}, u32[]{:S(2)}) async-start(f32[16,2,2,256]{3,2,1,0:T(2,128)} %copy.48), calls=%async_computation.1 | async-start | bytes 131072 | tf_op jit(solution)/shard_map/all_to_all | solution.py:75
  50.3 7.2 %all-to-all-done.1 = f32[16,2,2,256]{3,2,1,0:T(2,128)S(1)} async-done(((f32[16,2,2,256]{3,2,1,0:T(2,128)}), f32[16,2,2,256]{3,2,1,0:T(2,128)S(1)}, u32[]{:S(2)}, u32[]{:S(2)}) %all-to-all-start.1) | async-done | bytes 65568 | tf_op jit(solution)/shard_map/all_to_all | solution.py:75
  57.6 1.3 collective-permute-start
  58.9 3.0 %collective-permute-start.1 = (f32[2,1,512]{2,1,0:T(1,128)S(1)}, f32[2,1,512]{2,1,0:T(1,128)S(1)}, u32[]{:S(2)}, u32[]{:S(2)}) collective-permute-start(f32[2,1,512]{2,1,0:T(1,128)S(1)} %get-tuple-element.42), channel_id=1, source_target_pairs={{0,1},{2,3},{4,5},{6,7},{8,9},{10,11},{12,13},{14,15},{16,17},{18,... | collective-permute-start | bytes 12296 | tf_op jit(solution)/shard_map/ppermute | solution.py:25
  62.0 0.0 collective-permute-done
  62.0 0.8 collective-permute-done.1
  62.8 0.1 fusion.5
  62.9 1.3 collective-permute-start.2
  64.2 3.0 %collective-permute-start.3 = (f32[2,1,512]{2,1,0:T(1,128)S(1)}, f32[2,1,512]{2,1,0:T(1,128)S(1)}, u32[]{:S(2)}, u32[]{:S(2)}) collective-permute-start(f32[2,1,512]{2,1,0:T(1,128)S(1)} %get-tuple-element.38), channel_id=1, source_target_pairs={{0,1},{2,3},{4,5},{6,7},{8,9},{10,11},{12,13},{14,15},{16,17},{18,... | collective-permute-start | bytes 12296 | tf_op jit(solution)/shard_map/ppermute | solution.py:25
  67.2 0.0 collective-permute-done.2
  67.2 0.8 collective-permute-done.3
  68.0 0.1 fusion.9
  68.1 1.3 collective-permute-start.4
  69.4 3.2 %collective-permute-start.5 = (f32[2,1,512]{2,1,0:T(1,128)S(1)}, f32[2,1,512]{2,1,0:T(1,128)S(1)}, u32[]{:S(2)}, u32[]{:S(2)}) collective-permute-start(f32[2,1,512]{2,1,0:T(1,128)S(1)} %get-tuple-element.34), channel_id=1, source_target_pairs={{0,1},{2,3},{4,5},{6,7},{8,9},{10,11},{12,13},{14,15},{16,17},{18,... | collective-permute-start | bytes 12296 | tf_op jit(solution)/shard_map/ppermute | solution.py:25
  72.7 0.0 collective-permute-done.4
  72.7 0.6 collective-permute-done.5
  73.3 0.1 fusion.13
  73.5 4.4 %copy.51 = f32[1,2,2,4096]{2,1,0,3:T(2,128)} copy(f32[1,2,2,4096]{3,1,2,0:T(2,128)S(1)} %pad_maximum_fusion.1) | data formatting | bytes 131072 | tf_op jit(solution)/shard_map/stack | solution.py:93
  77.9 8.1 %reshape.253 = f32[16,1,1024]{2,1,0:T(1,128)} reshape(f32[4096,1,2,2]{3,2,1,0:T(2,128)} %bitcast.79) | data formatting | bytes 131072
  86.1 3.5 %all-to-all-start.2 = ((f32[16,1,1024]{2,1,0:T(1,128)}), f32[16,1,1024]{2,1,0:T(1,128)S(1)}, u32[]{:S(2)}, u32[]{:S(2)}) async-start(f32[16,1,1024]{2,1,0:T(1,128)} %reshape.253), calls=%async_computation.2 | async-start | bytes 131072 | tf_op jit(solution)/shard_map/all_to_all | solution.py:94
  89.6 7.5 %all-to-all-done.2 = f32[16,1,1024]{2,1,0:T(1,128)S(1)} async-done(((f32[16,1,1024]{2,1,0:T(1,128)}), f32[16,1,1024]{2,1,0:T(1,128)S(1)}, u32[]{:S(2)}, u32[]{:S(2)}) %all-to-all-start.2) | async-done | bytes 65568 | tf_op jit(solution)/shard_map/all_to_all | solution.py:94
  97.1 0.8 reduce.70
  97.9 7.7 %reshape.254 = f32[4096,1,2,2]{3,2,1,0:T(2,128)} reshape(f32[16,1024]{1,0:T(8,128)S(1)} %reduce.70) | data formatting | bytes 131072
  105.6 0.0 copy-start
  105.6 3.6 %copy.57 = f32[1,2,2,16,256]{4,3,2,1,0:T(8,128)S(1)} copy(f32[1,2,2,16,256]{2,1,4,3,0:T(2,128)} %bitcast.80) | data formatting | bytes 131072 | tf_op jit(solution)/shard_map/all_to_all | solution.py:94
  109.2 0.2 fusion.42
  109.5 0.2 fusion
  109.7 0.1 slice_reduce_fusion.2
  110.2 10.0 %all_to_all.54 = f32[16,1,2,256]{3,2,1,0:T(2,128)S(1)} all-to-all(f32[16,1,2,256]{3,2,1,0:T(2,128)S(1)} %constant_dynamic-update-slice_fusion), channel_id=1, replica_groups=mesh['tm'=16,'rows'=2] {'tm'}, dimensions={0} | all-to-all | bytes 65536 | tf_op jit(solution)/shard_map/all_to_all | solution.py:14
  120.2 0.1 slice_reduce_fusion
  120.3 2.6 %collective-permute-start.6 = (f32[2,8,512]{2,1,0:T(8,128)S(1)}, f32[2,8,512]{2,1,0:T(8,128)S(1)}, u32[]{:S(2)}, u32[]{:S(2)}) collective-permute-start(f32[2,8,512]{2,1,0:T(8,128)S(1)} %reshape_squeeze_reshape.3), channel_id=1, source_target_pairs={{0,2},{2,4},{4,6},{6,8},{8,10},{10,12},{12,14},{14,16},{16,18},{18... | collective-permute-start | bytes 98312 | tf_op jit(solution)/shard_map/ppermute | solution.py:34
  122.9 1.3 collective-permute-start.7
  124.2 3.0 %collective-permute-start.8 = (f32[1,1,512]{2,1,0:T(1,128)S(1)}, f32[1,1,512]{2,1,0:T(1,128)S(1)}, u32[]{:S(2)}, u32[]{:S(2)}) collective-permute-start(f32[1,1,512]{2,1,0:T(1,128)S(1)} %get-tuple-element.46), channel_id=1, source_target_pairs={{0,1},{2,3},{4,5},{6,7},{8,9},{10,11},{12,13},{14,15},{16,17},{18,... | collective-permute-start | bytes 6152 | tf_op jit(solution)/shard_map/ppermute | solution.py:25
  127.3 0.0 collective-permute-done.7
  127.3 0.8 collective-permute-done.8
  128.1 0.0 collective-permute-done.6
  128.1 0.1 fusion.26
  128.2 1.2 pad_maximum_fusion.18
  130.0 0.0 copy-done
  130.1 0.1 fusion.1
  130.2 0.1 pad_maximum_fusion.21
  130.3 0.6 broadcast_in_dim_reshape_squeeze_reshape.3
  130.9 39.0 %psum.7 = f32[5]{0:T(128)} all-reduce(f32[5]{0:T(128)S(1)} %pad_maximum_fusion.21), channel_id=1, replica_groups=mesh['tm'=16,'rows'=2] {'tm','rows'}, use_global_device_ids=true, to_apply=%region_2.3 | all-reduce | flops 5 | bytes 40 | tf_op jit(solution)/shard_map/psum | solution.py:116
  (67 shorter events, 0.8 us)
Async XLA Ops:
  46.5 11.0 %all-to-all-start.1 = ((f32[16,2,2,256]{3,2,1,0:T(2,128)}), f32[16,2,2,256]{3,2,1,0:T(2,128)S(1)}, u32[]{:S(2)}, u32[]{:S(2)}) async-start(f32[16,2,2,256]{3,2,1,0:T(2,128)} %copy.48), calls=%async_computation.1 | async-start | bytes 131072 | tf_op jit(solution)/shard_map/all_to_all | solution.py:75
  57.6 4.3 %collective-permute-start = (f32[2,1,512]{2,1,0:T(1,128)S(1)}, f32[2,1,512]{2,1,0:T(1,128)S(1)}, u32[]{:S(2)}, u32[]{:S(2)}) collective-permute-start(f32[2,1,512]{2,1,0:T(1,128)S(1)} %get-tuple-element.41), channel_id=1, source_target_pairs={{1,0},{3,2},{5,4},{7,6},{9,8},{11,10},{13,12},{15,14},{17,16},{19,... | collective-permute-start | bytes 12296 | tf_op jit(solution)/shard_map/ppermute | solution.py:26
  58.9 3.8 %collective-permute-start.1 = (f32[2,1,512]{2,1,0:T(1,128)S(1)}, f32[2,1,512]{2,1,0:T(1,128)S(1)}, u32[]{:S(2)}, u32[]{:S(2)}) collective-permute-start(f32[2,1,512]{2,1,0:T(1,128)S(1)} %get-tuple-element.42), channel_id=1, source_target_pairs={{0,1},{2,3},{4,5},{6,7},{8,9},{10,11},{12,13},{14,15},{16,17},{18,... | collective-permute-start | bytes 12296 | tf_op jit(solution)/shard_map/ppermute | solution.py:25
  62.9 4.3 %collective-permute-start.2 = (f32[2,1,512]{2,1,0:T(1,128)S(1)}, f32[2,1,512]{2,1,0:T(1,128)S(1)}, u32[]{:S(2)}, u32[]{:S(2)}) collective-permute-start(f32[2,1,512]{2,1,0:T(1,128)S(1)} %get-tuple-element.37), channel_id=1, source_target_pairs={{1,0},{3,2},{5,4},{7,6},{9,8},{11,10},{13,12},{15,14},{17,16},{19,... | collective-permute-start | bytes 12296 | tf_op jit(solution)/shard_map/ppermute | solution.py:26
  64.2 3.8 %collective-permute-start.3 = (f32[2,1,512]{2,1,0:T(1,128)S(1)}, f32[2,1,512]{2,1,0:T(1,128)S(1)}, u32[]{:S(2)}, u32[]{:S(2)}) collective-permute-start(f32[2,1,512]{2,1,0:T(1,128)S(1)} %get-tuple-element.38), channel_id=1, source_target_pairs={{0,1},{2,3},{4,5},{6,7},{8,9},{10,11},{12,13},{14,15},{16,17},{18,... | collective-permute-start | bytes 12296 | tf_op jit(solution)/shard_map/ppermute | solution.py:25
  68.1 4.5 %collective-permute-start.4 = (f32[2,1,512]{2,1,0:T(1,128)S(1)}, f32[2,1,512]{2,1,0:T(1,128)S(1)}, u32[]{:S(2)}, u32[]{:S(2)}) collective-permute-start(f32[2,1,512]{2,1,0:T(1,128)S(1)} %get-tuple-element.33), channel_id=1, source_target_pairs={{1,0},{3,2},{5,4},{7,6},{9,8},{11,10},{13,12},{15,14},{17,16},{19,... | collective-permute-start | bytes 12296 | tf_op jit(solution)/shard_map/ppermute | solution.py:26
  69.4 3.8 %collective-permute-start.5 = (f32[2,1,512]{2,1,0:T(1,128)S(1)}, f32[2,1,512]{2,1,0:T(1,128)S(1)}, u32[]{:S(2)}, u32[]{:S(2)}) collective-permute-start(f32[2,1,512]{2,1,0:T(1,128)S(1)} %get-tuple-element.34), channel_id=1, source_target_pairs={{0,1},{2,3},{4,5},{6,7},{8,9},{10,11},{12,13},{14,15},{16,17},{18,... | collective-permute-start | bytes 12296 | tf_op jit(solution)/shard_map/ppermute | solution.py:25
  86.1 11.0 %all-to-all-start.2 = ((f32[16,1,1024]{2,1,0:T(1,128)}), f32[16,1,1024]{2,1,0:T(1,128)S(1)}, u32[]{:S(2)}, u32[]{:S(2)}) async-start(f32[16,1,1024]{2,1,0:T(1,128)} %reshape.253), calls=%async_computation.2 | async-start | bytes 131072 | tf_op jit(solution)/shard_map/all_to_all | solution.py:94
  105.6 24.4 %copy-start = (f32[4,2,1,8,512]{4,3,2,1,0:T(8,128)S(1)}, f32[4,2,1,8,512]{4,3,2,1,0:T(8,128)}, u32[]{:S(2)}) copy-start(f32[4,2,1,8,512]{4,3,2,1,0:T(8,128)} %param.3) | copy-start | bytes 393220
  120.3 7.8 %collective-permute-start.6 = (f32[2,8,512]{2,1,0:T(8,128)S(1)}, f32[2,8,512]{2,1,0:T(8,128)S(1)}, u32[]{:S(2)}, u32[]{:S(2)}) collective-permute-start(f32[2,8,512]{2,1,0:T(8,128)S(1)} %reshape_squeeze_reshape.3), channel_id=1, source_target_pairs={{0,2},{2,4},{4,6},{6,8},{8,10},{10,12},{12,14},{14,16},{16,18},{18... | collective-permute-start | bytes 98312 | tf_op jit(solution)/shard_map/ppermute | solution.py:34
  122.9 4.4 %collective-permute-start.7 = (f32[1,1,512]{2,1,0:T(1,128)S(1)}, f32[1,1,512]{2,1,0:T(1,128)S(1)}, u32[]{:S(2)}, u32[]{:S(2)}) collective-permute-start(f32[1,1,512]{2,1,0:T(1,128)S(1)} %get-tuple-element.45), channel_id=1, source_target_pairs={{1,0},{3,2},{5,4},{7,6},{9,8},{11,10},{13,12},{15,14},{17,16},{19,... | collective-permute-start | bytes 6152 | tf_op jit(solution)/shard_map/ppermute | solution.py:26
  124.2 3.8 %collective-permute-start.8 = (f32[1,1,512]{2,1,0:T(1,128)S(1)}, f32[1,1,512]{2,1,0:T(1,128)S(1)}, u32[]{:S(2)}, u32[]{:S(2)}) collective-permute-start(f32[1,1,512]{2,1,0:T(1,128)S(1)} %get-tuple-element.46), channel_id=1, source_target_pairs={{0,1},{2,3},{4,5},{6,7},{8,9},{10,11},{12,13},{14,15},{16,17},{18,... | collective-permute-start | bytes 6152 | tf_op jit(solution)/shard_map/ppermute | solution.py:25
